TPU v7x, 32 devices: a whole 2x2x4 slice. The times are simulated.
32 devices in a mesh: dp: 8 (over z, x), tensor: 4 (over y, core).
Axes of the slice: x: 2, y: 2, z: 4, core: 2. Of those that a mesh axis runs over, the one named last changes fastest.
Arguments:
- tokens: bfloat16 [8, 256, 4096], P('dp', 'tensor'), may hold values from -6 to 6
- gain: bfloat16 [4096], replicated, may hold values from 0.5 to 1.5
- wq: bfloat16 [4096, 4096], P(None, 'tensor'), may hold values from -0.09375 to 0.09375
- bq: bfloat16 [4096], P('tensor'), may hold values from -5 to 5
- wkv: bfloat16 [4096, 1024], P(None, 'tensor'), may hold values from -0.09375 to 0.09375
- bkv: bfloat16 [1024], P('tensor'), may hold values from -5 to 5
- wo: bfloat16 [4096, 4096], P('tensor'), may hold values from -0.375 to 0.375
- check_weights: float32 [8, 256], P('dp'), may hold values from -12 to 12
Outputs:
- attended: bfloat16 [8, 256, 4096], P('dp', 'tensor')
- checksum: float32 [4096], replicated
All inputs are finite; a program needn't handle non-finite values.
Results may differ from a plain program's by a relative error of at most 0.018.
Values may be sent and summed in bfloat16 or wider, within the bound.
A program may use at most 64 MiB of HBM per device.

v0:
```python
import jax
import jax.numpy as jnp
from jax import lax
from jax.sharding import PartitionSpec as P

HEADS = 32
KV = 4
HD = 128


EPS = 1e-06
THETA = 1000000.0


def rope(values, head_size):
    rows = values.shape[0]
    half = head_size // 2
    inverse = THETA ** (-(jnp.arange(half, dtype=jnp.float32) * 2.0 / head_size))
    angles = jnp.arange(rows, dtype=jnp.float32)[:, None] * inverse[None, :]
    cosine = jnp.cos(angles)[:, None, :]
    sine = jnp.sin(angles)[:, None, :]
    shaped = values.reshape(rows, -1, head_size)
    first = shaped[..., :half]
    second = shaped[..., half:]
    turned = jnp.concatenate(
        [first * cosine - second * sine, second * cosine + first * sine], axis=-1
    )
    return turned.reshape(rows, -1)


def local(tokens, gain, wq, bq, wkv, bkv, wo, check_weights):
    states = tokens[0].astype(jnp.float32)
    normed = (
        states
        * lax.rsqrt(jnp.mean(states * states, axis=-1, keepdims=True) + EPS)
        * gain.astype(jnp.float32)
    ).astype(jnp.bfloat16)
    position = lax.axis_index("tensor")
    head_dev = wq.shape[1] // HD
    query_cols = head_dev * HD
    shared = position * head_dev // (HEADS // KV)
    joined_w = jnp.concatenate([wq, wkv], axis=1)
    joined_b = jnp.concatenate([bq, bkv], axis=0).astype(jnp.float32)
    projected = (
        jnp.dot(
            lax.all_gather(normed, "tensor", axis=0, tiled=True),
            joined_w,
            preferred_element_type=jnp.float32,
        )
        + joined_b[None, :]
    )
    seq_rows = projected.shape[0]
    query = rope(projected[:, :query_cols], HD).astype(jnp.bfloat16)
    kv_local = projected[:, query_cols:].astype(jnp.bfloat16)
    kv_whole = lax.all_gather(kv_local, "tensor", axis=1, tiled=True)
    key_part = lax.dynamic_slice_in_dim(kv_whole, shared * HD, HD, 1)
    values = lax.dynamic_slice_in_dim(kv_whole, KV * HD + shared * HD, HD, 1)
    keys = rope(key_part.astype(jnp.float32), HD).astype(jnp.bfloat16)
    scale = HD ** (-0.5)
    block = min(512, seq_rows)
    query_heads = query.reshape(seq_rows, head_dev, HD)
    pieces = []
    for number in range(seq_rows // block):
        stop = (number + 1) * block
        query_block = query_heads[number * block : stop]
        scores = (
            jnp.einsum("qhd,kd->hqk", query_block, keys[:stop], preferred_element_type=jnp.float32)
            * scale
        )
        allowed = jnp.arange(block)[:, None] + number * block >= jnp.arange(stop)[None, :]
        scores = jnp.where(allowed[None, :, :], scores, -1e30)
        probs = jax.nn.softmax(scores, axis=-1).astype(jnp.bfloat16)
        mixed = jnp.einsum(
            "hqk,kd->qhd", probs, values[:stop], preferred_element_type=jnp.float32
        ).astype(jnp.bfloat16)
        pieces.append(mixed.reshape(block, query_cols))
    context = jnp.concatenate(pieces, axis=0)
    summed = lax.psum_scatter(
        jnp.dot(context, wo, preferred_element_type=jnp.float32).astype(jnp.bfloat16),
        "tensor",
        scatter_dimension=0,
        tiled=True,
    )
    attended = summed[None, :, :]
    summary = jnp.dot(
        check_weights[0], context.astype(jnp.float32), precision=lax.Precision.HIGHEST
    )
    term = jnp.dot(summary, wo.astype(jnp.float32), precision=lax.Precision.HIGHEST)
    total = lax.psum(term, ("dp", "tensor"))
    checksum = total / jnp.sqrt(jnp.float32(seq_rows * lax.axis_size("dp")))
    return (attended, checksum)


def solution(mesh):
    placed = (
        P("dp", "tensor", None),
        P(),
        P(None, "tensor"),
        P("tensor"),
        P(None, "tensor"),
        P("tensor"),
        P("tensor", None),
        P("dp", None),
    )
    return jax.shard_map(
        local, mesh=mesh, in_specs=placed, out_specs=(P("dp", "tensor", None), P()), check_vma=False
    )
```

profile of v0, /device:TPU:0, one launch (start us, length us, event | category | flops | bytes accessed | tf_op | source)
XLA Modules:
  0.0 118.1 jit_solution(9520385289400516932)
XLA Ops:
  7.2 0.0 copy-start
  7.2 0.0 copy-start.1
  7.2 0.0 copy-start.2
  7.2 0.0 copy-start.3
  7.2 0.0 all-gather.2.cloned.1.call-start
  7.3 0.8 convert_element_type.43
  8.1 1.2 %fusion.9 = f32[64]{0:T(128)S(1)} fusion(bf16[1,64,4096]{2,1,0:T(8,128)(2,1)} %param.8), kind=kLoop, calls=%fused_computation.15 | loop fusion | flops 786368 | bytes 524544 | tf_op jit(solution)/shard_map/reduce_sum | solution.py:35
  9.4 2.0 %fusion.11 = bf16[64,4096]{1,0:T(8,128)(2,1)} fusion(bf16[1,64,4096]{2,1,0:T(8,128)(2,1)} %param.8, f32[4096]{0:T(1024)S(1)} %convert_element_type.43, f32[64]{0:T(128)S(1)} %add_rsqrt_fusion), kind=kLoop, calls=%fused_computation.17 | loop fusion | flops 1048576 | bytes 1065216 | tf_op jit(solution)/shard_map/convert_element_type | solution.py:37
  11.4 0.0 all-gather.2.cloned.1.call-update
  11.4 0.0 reduce-scatter.2.cloned.1.call-start
  11.5 0.0 copy-done.1
  11.5 0.0 copy-done.2
  11.6 0.5 fusion.24
  12.1 24.8 %all-gather.2.cloned.1.call-done = bf16[256,4096]{1,0:T(8,128)(2,1)} async-done(((bf16[64,4096]{1,0:T(8,128)(2,1)}), bf16[256,4096]{1,0:T(8,128)(2,1)}) %all-gather.2.cloned.1.call-update) | async-done | bytes 2097168 | tf_op jit(solution)/shard_map/all_gather | solution.py:46
  36.9 0.0 copy-done.3
  36.9 7.5 %fusion.5 = f32[256,1280]{1,0:T(8,128)S(1)} fusion(bf16[256,4096]{1,0:T(8,128)(2,1)} %all-gather.2.cloned.1.call-done, bf16[4096,256]{1,0:T(8,128)(2,1)S(1)} %copy-done.3, bf16[4096,1024]{1,0:T(8,128)(2,1)} %param.10, f32[1280]{0:T(1024)S(1)} %maximum_convert_fusion), kind=kOutput, calls=%fused_computation.6 | convolution fusion | flops 2705653760 | bytes 13898752 | tf_op jit(solution)/shard_map/dot_general | solution.py:45
  44.4 0.1 slice_bitcast_fusion
  44.5 7.2 %all_gather.7 = bf16[256,1024]{1,0:T(8,128)(2,1)S(1)} all-gather(bf16[256,256]{1,0:T(8,128)(2,1)S(1)} %slice.37), channel_id=1, replica_groups=mesh['dp'=8,'tensor'=4] {'tensor'}, dimensions={1}, use_global_device_ids=true | all-gather | bytes 655360 | tf_op jit(solution)/shard_map/all_gather | solution.py:55
  51.7 0.5 subtract_convert_fusion.1
  52.3 0.2 copy.19
  52.5 0.3 fusion.39
  52.8 0.4 subtract_convert_fusion
  53.2 2.4 %fusion.40 = (f32[8,256]{1,0:T(8,128)S(1)}, f32[8,256,256]{1,2,0:T(8,128)}) fusion(pred[256,256]{0,1:T(8,128)(4,1)S(1)} %iota_compare_fusion, bf16[256,8,64]{2,0,1:T(8,128)(2,1)S(1)} %get-tuple-element.3, bf16[256,8,64]{2,0,1:T(8,128)(2,1)S(1)} %get-tuple-element.2, bf16[256,1,64]{2,0,1:T(8,128)(2,1)S(1)} %get-tuple-element.7, ...), kind=kOutput, calls=%fused_computation.54 | convolution fusion | flops 137494784 | bytes 2760704 | tf_op jit(solution)/shard_map/sub | solution.py:72
  55.6 1.9 %convolution_convert_fusion.1 = bf16[128,8,256]{2,0,1:T(8,128)(2,1)S(1)} fusion(f32[8,256,256]{1,2,0:T(8,128)} %get-tuple-element.11, f32[8,256]{1,0:T(8,128)S(1)} %get-tuple-element.10, bf16[256,1024]{1,0:T(8,128)(2,1)S(1)} %all_gather.7, s32[]{:T(128)S(6)} %select_n.16), kind=kOutput, calls=%fused_computation.13 | convolution fusion | flops 135528448 | bytes 2695172 | tf_op jit(solution)/shard_map/hqk,kd->qhd/dot_general | solution.py:73
  57.5 7.1 %convolution_convert_fusion = bf16[256,4096]{1,0:T(8,128)(2,1)} fusion(bf16[256,1024]{0,1:T(8,128)(2,1)S(1)} %bitcast.49, bf16[1024,4096]{1,0:T(8,128)(2,1)} %param.14), kind=kOutput, calls=%fused_computation.5 | convolution fusion | flops 2148532224 | bytes 11010048 | tf_op jit(solution)/shard_map/dot_general | solution.py:79
  64.6 0.0 reduce-scatter.2.cloned.1.call-update
  64.7 0.0 copy-done
  64.7 0.5 convolution_bitcast_fusion
  65.2 5.7 %fusion.43 = f32[1,4096]{1,0:T(1,128)S(1)} fusion(f32[1024,1]{0,1:T(1,128)S(1)} %convolution_bitcast_fusion, bf16[1024,4096]{1,0:T(8,128)(2,1)} %param.14), kind=kOutput, calls=%fused_computation.55 | convolution fusion | flops 50331648 | bytes 8409088 | tf_op jit(solution)/shard_map/dot_general | solution.py:88
  70.9 39.7 %psum.7 = f32[4096]{0:T(1024)S(1)} all-reduce(f32[4096]{0:T(1024)S(1)} %bitcast.51), channel_id=1, replica_groups=mesh['dp'=8,'tensor'=4] {'dp','tensor'}, use_global_device_ids=true, to_apply=%region_4.5 | all-reduce | flops 4096 | bytes 32768 | tf_op jit(solution)/shard_map/psum | solution.py:89
  110.6 0.6 broadcast_multiply_fusion
  111.2 0.0 reduce-scatter.2.cloned.1.call-done
  (6 shorter events, 0.1 us)
Async XLA Ops:
  7.2 57.5 %copy-start = (f32[1,256]{1,0:T(1,128)S(1)}, f32[1,256]{1,0:T(1,128)}, u32[]{:S(2)}) copy-start(f32[1,256]{1,0:T(1,128)} %param.15) | copy-start | bytes 3076
  7.2 4.3 %copy-start.1 = (bf16[1024]{0:T(1024)(128)(2,1)S(1)}, bf16[1024]{0:T(1024)(128)(2,1)}, u32[]{:S(2)}) copy-start(bf16[1024]{0:T(1024)(128)(2,1)} %param.11) | copy-start | bytes 6148
  7.2 4.3 %copy-start.2 = (bf16[256]{0:T(256)(128)(2,1)S(1)}, bf16[256]{0:T(256)(128)(2,1)}, u32[]{:S(2)}) copy-start(bf16[256]{0:T(256)(128)(2,1)} %param.13) | copy-start | bytes 1540
  7.2 29.7 %copy-start.3 = (bf16[4096,256]{1,0:T(8,128)(2,1)S(1)}, bf16[4096,256]{1,0:T(8,128)(2,1)}, u32[]{:S(2)}) copy-start(bf16[4096,256]{1,0:T(8,128)(2,1)} %param.12) | copy-start | bytes 6291460
  7.2 29.7 %all-gather.2.cloned.1.call-start = ((), (), s32[]{:S(2)}) async-start(), calls=%async_computation.1 | async-start | bytes 2621440 | tf_op jit(solution)/shard_map/all_gather | solution.py:46
  11.4 99.8 %reduce-scatter.2.cloned.1.call-start = ((), (), s32[]{:S(2)}) async-start(), calls=%async_computation.2 | async-start | bytes 2621440 | tf_op jit(solution)/shard_map/reduce_scatter | solution.py:78
Sparse Core Ops, SparseCore 0:
  11.5 25.2 all-gather.1
  64.8 31.3 reduce-scatter.1
where the time goes:
time: 118 us
  blocking collectives  46.9 us (40%)
  matrix products  25.1 us (21%)
  waiting for transfers between devices  24.8 us (21%)
  between operations  14.2 us (12%)
  other arithmetic  6.25 us (5%)
    psum x1, blocking collectives, local(): total = lax.psum(term, ('dp', 'tensor'))  39.7 us
    all_gather x1, waiting for transfers between devices, local(): lax.all_gather(normed, 'tensor', axis=0, tiled=True)  24.8 us
    dot_general x1, matrix products, local(): jnp.dot(lax.all_gather(normed, 'tensor', axis=0, tiled=True), joined_w, p...  7.53 us
    all_gather x1, blocking collectives, local(): kv_whole = lax.all_gather(kv_local, 'tensor', axis=1, tiled=True)  7.16 us
    dot_general x1, matrix products, local(): jnp.dot(context, wo, preferred_element_type=jnp.float32)  7.11 us
    dot_general x1, matrix products, local(): jnp.dot(summary, wo.astype(jnp.float32), precision=lax.Precision.HIGHEST)  5.68 us
  transfers between devices with their start and end apart: 2, of which 1 were waited for; matrix products, arithmetic and copies ran while one was open for 6% of the time, Pallas kernels for 0%

commit v1 on v0

--- a/solution.py
+++ b/solution.py
@@ -1,6 +1,11 @@
+import functools
+
 import jax
 import jax.numpy as jnp
+import numpy as np
 from jax import lax
+from jax.experimental import pallas as pl
+from jax.experimental.pallas import tpu as pltpu
 from jax.sharding import PartitionSpec as P
 
 HEADS = 32
@@ -10,6 +15,9 @@
 
 EPS = 1e-06
 THETA = 1000000.0
+MESH = pl.DeviceIdType.MESH
+F32 = jnp.float32
+BF16 = jnp.bfloat16
 
 
 def rope(values, head_size):
@@ -28,7 +36,7 @@
     return turned.reshape(rows, -1)
 
 
-def local(tokens, gain, wq, bq, wkv, bkv, wo, check_weights):
+def general(tokens, gain, wq, bq, wkv, bkv, wo, check_weights):
     states = tokens[0].astype(jnp.float32)
     normed = (
         states
@@ -85,10 +93,395 @@
     summary = jnp.dot(
         check_weights[0], context.astype(jnp.float32), precision=lax.Precision.HIGHEST
     )
+    summary = lax.psum(summary, "dp")
     term = jnp.dot(summary, wo.astype(jnp.float32), precision=lax.Precision.HIGHEST)
-    total = lax.psum(term, ("dp", "tensor"))
+    total = lax.psum(term, "tensor")
     checksum = total / jnp.sqrt(jnp.float32(seq_rows * lax.axis_size("dp")))
     return (attended, checksum)
+
+
+def split3(row, count=16):
+    high = row.astype(BF16).astype(F32)
+    rest = row - high
+    middle = rest.astype(BF16).astype(F32)
+    low = rest - middle
+    index = lax.broadcasted_iota(jnp.int32, (count, row.shape[1]), 0)
+    wide = (count, row.shape[1])
+    rows = jnp.where(
+        index == 0,
+        jnp.broadcast_to(high, wide),
+        jnp.where(
+            index == 1,
+            jnp.broadcast_to(middle, wide),
+            jnp.where(index == 2, jnp.broadcast_to(low, wide), 0.0),
+        ),
+    )
+    return rows.astype(BF16)
+
+
+def fused_kernel(
+    ndp, kc, nc,
+    tok, gain, wq, bq, wkv, bkv, wo, cw, cos, sin,
+    out, chk,
+    xs, ws, wos, acc, coss, sins, kvl, kvd, keys, ctx, ctxp,
+    p_s, p_r, f_s, f_r, q_s, q_r, keep, mine, sum_s, sum_r, term_s, term_r,
+    w_sem, wo_sem, t_sem, far_s, far_r, near_s, near_r, fwd_s, fwd_r, kv_s, kv_r,
+    ps_s, ps_r, fs_s, fs_r, qs_s, qs_r, sm_s, sm_r, tm_s, tm_r,
+):
+    rows, d = tok.shape
+    pair = 2 * rows
+    seq = 2 * pair
+    qcols = wq.shape[1]
+    heads = qcols // HD
+    kch = d // kc
+    nch = d // nc
+    me = lax.axis_index("tensor")
+    dp = lax.axis_index("dp")
+    chip = me // 2
+    core = me % 2
+    partner = chip * 2 + (1 - core)
+    across = (1 - chip) * 2 + core
+    diagonal = (1 - chip) * 2 + (1 - core)
+
+    def rows_of(device):
+        return pl.ds(pl.multiple_of(device * rows, rows), rows)
+
+    own_rows = pl.ds(pl.multiple_of(chip * pair, pair), pair)
+    other_rows = pl.ds(pl.multiple_of((1 - chip) * pair, pair), pair)
+
+    barrier = pltpu.get_barrier_semaphore()
+    for peer in (partner, across, diagonal):
+        pl.semaphore_signal(barrier, inc=1, device_id={"tensor": peer}, device_id_type=MESH)
+    for step in range(1, ndp):
+        pl.semaphore_signal(
+            barrier, inc=1, device_id={"dp": (dp + step) % ndp}, device_id_type=MESH
+        )
+
+    def load_q(k):
+        at = pl.ds(k * kch, kch)
+        return pltpu.make_async_copy(wq.at[at, :], ws.at[k, :, pl.ds(0, qcols)], w_sem.at[0, k])
+
+    def load_kv(k):
+        at = pl.ds(k * kch, kch)
+        return pltpu.make_async_copy(
+            wkv.at[at, :], ws.at[k, :, pl.ds(qcols, wkv.shape[1])], w_sem.at[1, k]
+        )
+
+    def load_o(n):
+        at = pl.ds(n * nch, nch)
+        return pltpu.make_async_copy(wo.at[:, at], wos.at[n], wo_sem.at[n])
+
+    for k in range(kc):
+        load_q(k).start()
+        load_kv(k).start()
+    load_cos = pltpu.make_async_copy(cos, coss, t_sem.at[0])
+    load_sin = pltpu.make_async_copy(sin, sins, t_sem.at[1])
+    load_cos.start()
+    load_sin.start()
+    for n in range(nc):
+        load_o(n).start()
+
+    square = jnp.zeros((rows, kch), F32)
+    for k in range(kc):
+        part = tok[:, k * kch : (k + 1) * kch].astype(F32)
+        square = square + part * part
+    inverse = lax.rsqrt(jnp.sum(square, axis=-1, keepdims=True) / d + EPS)
+    for k in range(kc):
+        part = tok[:, k * kch : (k + 1) * kch].astype(F32)
+        scaled = part * inverse * gain[:, k * kch : (k + 1) * kch].astype(F32)
+        xs[k, rows_of(me), :] = scaled.astype(BF16)
+
+    pl.semaphore_wait(barrier, 3 + ndp - 1)
+
+    def remote(src, dst, send, recv, peer):
+        return pltpu.make_async_remote_copy(
+            src_ref=src, dst_ref=dst, send_sem=send, recv_sem=recv,
+            device_id={"tensor": peer}, device_id_type=MESH,
+        )
+
+    def far(k, block):
+        at = xs.at[k, rows_of(block), :]
+        return remote(at, at, far_s.at[k], far_r.at[k], across)
+
+    def near(k, block):
+        at = xs.at[k, rows_of(block), :]
+        return remote(at, at, near_s.at[k], near_r.at[k], partner)
+
+    def forward(k, block):
+        at = xs.at[k, rows_of(block), :]
+        return remote(at, at, fwd_s.at[k], fwd_r.at[k], partner)
+
+    for k in range(kc):
+        near(k, me).start()
+        far(k, me).start()
+
+    def project(k, at, first):
+        product = jnp.dot(xs[k, at, :], ws[k], preferred_element_type=F32)
+        if first:
+            acc[at, :] = product
+        else:
+            acc[at, :] += product
+
+    def own_step(k, first):
+        load_q(k).wait()
+        load_kv(k).wait()
+        near(k, partner).wait_recv()
+        project(k, own_rows, first)
+
+    own_step(0, True)
+
+    @pl.loop(1, kc)
+    def _(k):
+        own_step(k, False)
+
+    kinds = wkv.shape[1] // HD
+
+    def kv_copy(slot, half):
+        number = me * kinds + slot
+        at = pl.ds(pl.multiple_of(half * pair, pair), pair)
+        return remote(
+            kvl.at[slot, at, :], kvd.at[number // KV, at, :],
+            kv_s.at[slot, half], kv_r.at[number // KV, half], number % KV,
+        )
+
+    def kv_wait(kind, half):
+        at = pl.ds(pl.multiple_of(half * pair, pair), pair)
+        here = kvd.at[kind, at, :]
+        return remote(here, here, kv_s.at[0, half], kv_r.at[kind, half], partner)
+
+    def kv_send(half):
+        at = pl.ds(pl.multiple_of(half * pair, pair), pair)
+        for slot in range(kinds):
+            lanes = slice(qcols + slot * HD, qcols + (slot + 1) * HD)
+            bias = bkv[:, slot * HD : (slot + 1) * HD].astype(F32)
+            kvl[slot, at, :] = (acc[at, lanes] + bias).astype(BF16)
+        for slot in range(kinds):
+            number = me * kinds + slot
+
+            @pl.when(number % KV != me)
+            def _():
+                kv_copy(slot, half).start()
+
+            @pl.when(number % KV == me)
+            def _():
+                kvd[number // KV, at, :] = kvl[slot, at, :]
+
+    kv_send(chip)
+
+    for k in range(kc + 1):
+        if k < kc:
+            far(k, across).wait_recv()
+            forward(k, across).start()
+        if k > 0:
+            forward(k - 1, diagonal).wait_recv()
+            project(k - 1, other_rows, k == 1)
+    kv_send(1 - chip)
+
+    load_cos.wait()
+    load_sin.wait()
+    shared = me * heads // (HEADS // KV)
+    for kind in range(2):
+        source = (kind * KV + shared) // kinds
+
+        @pl.when(source != me)
+        def _():
+            for half in range(2):
+                kv_wait(kind, half).wait_recv()
+
+    raw = kvd[0, :, :].astype(F32)
+    keys[...] = (raw * coss[...] + pltpu.roll(raw, HD // 2, 1) * sins[...]).astype(BF16)
+
+    scale = HD ** (-0.5)
+    for h in range(heads):
+        lanes = slice(h * HD, (h + 1) * HD)
+        for block in range(2):
+            at = slice(block * pair, (block + 1) * pair)
+            stop = (block + 1) * pair
+            query = acc[at, lanes] + bq[:, lanes].astype(F32)
+            query = query * coss[at, :] + pltpu.roll(query, HD // 2, 1) * sins[at, :]
+            scores = lax.dot_general(
+                query.astype(BF16), keys[:stop, :], (((1,), (1,)), ((), ())),
+                preferred_element_type=F32,
+            ) * scale
+            down = lax.broadcasted_iota(jnp.int32, scores.shape, 0) + block * pair
+            right = lax.broadcasted_iota(jnp.int32, scores.shape, 1)
+            scores = jnp.where(down >= right, scores, -1e30)
+            raised = jnp.exp(scores - jnp.max(scores, axis=-1, keepdims=True))
+            total = jnp.sum(raised, axis=-1, keepdims=True)
+            mixed = jnp.dot(raised.astype(BF16), kvd[1, :stop, :], preferred_element_type=F32)
+            mixed = (mixed * (1.0 / total)).astype(BF16)
+            ctx[at, lanes] = mixed
+            same = 1 - (block - chip) * (block - chip)
+            for side in range(2):
+                place = 2 * same + 1 - (side - core) * (side - core)
+                ctxp[rows_of(place), lanes] = mixed[side * rows : (side + 1) * rows, :]
+
+    def p_copy(n):
+        return remote(p_s.at[n], p_r.at[n], ps_s.at[n], ps_r.at[n], partner)
+
+    def f_copy(n):
+        return remote(f_s.at[n], f_r.at[n], fs_s.at[n], fs_r.at[n], across)
+
+    def q_copy(n):
+        return remote(q_s.at[n], q_r.at[n], qs_s.at[n], qs_r.at[n], partner)
+
+    def cross(n):
+        p_copy(n).wait_recv()
+        f_s[n] = (keep[n] + p_r[n].astype(F32)).astype(BF16)
+        f_copy(n).start()
+
+    def first_part(n):
+        load_o(n).wait()
+        product = jnp.dot(ctxp[:pair, :], wos[n], preferred_element_type=F32)
+        p_s[n] = product[:rows].astype(BF16)
+        p_copy(n).start()
+        keep[n] = product[rows:]
+
+    first_part(0)
+
+    @pl.loop(1, nc)
+    def _(n):
+        first_part(n)
+        cross(n - 1)
+
+    weighted = jnp.dot(split3(cw[...]), ctx[...], preferred_element_type=F32)
+    summary = jnp.sum(weighted, axis=0, keepdims=True)
+    sum_s[...] = summary
+    sum_r[dp] = summary
+    cross(nc - 1)
+
+    def sum_copy(peer, owner):
+        return pltpu.make_async_remote_copy(
+            src_ref=sum_s, dst_ref=sum_r.at[owner], send_sem=sm_s.at[peer],
+            recv_sem=sm_r.at[owner], device_id={"dp": peer}, device_id_type=MESH,
+        )
+
+    for step in range(1, ndp):
+        sum_copy((dp + step) % ndp, dp).start()
+
+    @pl.loop(0, nc)
+    def _(n):
+        product = jnp.dot(ctxp[pair:, :], wos[n], preferred_element_type=F32)
+        q_s[n] = product[:rows].astype(BF16)
+        q_copy(n).start()
+        mine[n] = product[rows:]
+
+    for step in range(1, ndp):
+        peer = (dp + step) % ndp
+        sum_copy(peer, peer).wait_recv()
+    whole = sum_r[0]
+    for index in range(1, ndp):
+        whole = whole + sum_r[index]
+    three = split3(whole)
+    for n in range(nc):
+        lanes = slice(n * nch, (n + 1) * nch)
+        product = jnp.dot(three, wos[n], preferred_element_type=F32)
+        term = jnp.sum(product, axis=0, keepdims=True)
+        term_s[:, lanes] = term
+        term_r[me, :, lanes] = term
+
+    def term_copy(peer, owner):
+        return remote(term_s, term_r.at[owner], tm_s.at[peer], tm_r.at[owner], peer)
+
+    for peer in (partner, across, diagonal):
+        term_copy(peer, me).start()
+
+    for n in range(nc):
+        lanes = slice(n * nch, (n + 1) * nch)
+        q_copy(n).wait_recv()
+        f_copy(n).wait_recv()
+        out[:, lanes] = (mine[n] + q_r[n].astype(F32) + f_r[n].astype(F32)).astype(BF16)
+
+    for peer in (partner, across, diagonal):
+        term_copy(peer, peer).wait_recv()
+    size = np.float32(1.0) / np.sqrt(np.float32(seq * ndp))
+    total = term_r[0] + term_r[1] + term_r[2] + term_r[3]
+    chk[...] = total * size
+
+    for k in range(kc):
+        near(k, me).wait_send()
+        far(k, me).wait_send()
+        forward(k, across).wait_send()
+    for slot in range(kinds):
+        for half in range(2):
+
+            @pl.when((me * kinds + slot) % KV != me)
+            def _():
+                kv_copy(slot, half).wait_send()
+
+    for n in range(nc):
+        p_copy(n).wait_send()
+        f_copy(n).wait_send()
+        q_copy(n).wait_send()
+    for step in range(1, ndp):
+        sum_copy((dp + step) % ndp, dp).wait_send()
+    for peer in (partner, across, diagonal):
+        term_copy(peer, me).wait_send()
+
+
+def tables(seq):
+    half = HD // 2
+    inverse = THETA ** (-(np.arange(half, dtype=np.float32) * np.float32(2.0) / np.float32(HD)))
+    angles = np.arange(seq, dtype=np.float32)[:, None] * inverse[None, :].astype(np.float32)
+    cosine = np.cos(angles).astype(np.float32)
+    sine = np.sin(angles).astype(np.float32)
+    return (
+        np.concatenate([cosine, cosine], axis=1),
+        np.concatenate([-sine, sine], axis=1),
+    )
+
+
+def fused(ndp, n_tensor, tokens, gain, wq, bq, wkv, bkv, wo, check_weights):
+    rows, d = tokens.shape[1:]
+    seq = rows * n_tensor
+    kc = nc = 8
+    kch, nch = d // kc, d // nc
+    qcols, kvcols = wq.shape[1], wkv.shape[1]
+    cosine, sine = tables(seq)
+    vmem = pl.BlockSpec(memory_space=pltpu.VMEM)
+    hbm = pl.BlockSpec(memory_space=pl.ANY)
+    dma = pltpu.SemaphoreType.DMA
+    block = pltpu.VMEM((nc, rows, nch), BF16)
+    wide = pltpu.VMEM((nc, rows, nch), F32)
+    attended, checksum = pl.pallas_call(
+        functools.partial(fused_kernel, ndp, kc, nc),
+        out_shape=(
+            jax.ShapeDtypeStruct((rows, d), BF16),
+            jax.ShapeDtypeStruct((1, d), F32),
+        ),
+        in_specs=[vmem, vmem, hbm, vmem, hbm, vmem, hbm, vmem, hbm, hbm],
+        out_specs=(vmem, vmem),
+        scratch_shapes=[
+            pltpu.VMEM((kc, seq, kch), BF16),
+            pltpu.VMEM((kc, kch, qcols + kvcols), BF16),
+            pltpu.VMEM((nc, qcols, nch), BF16),
+            pltpu.VMEM((seq, qcols + kvcols), F32),
+            pltpu.VMEM((seq, HD), F32),
+            pltpu.VMEM((seq, HD), F32),
+            pltpu.VMEM((kvcols // HD, seq, HD), BF16),
+            pltpu.VMEM((2, seq, HD), BF16),
+            pltpu.VMEM((seq, HD), BF16),
+            pltpu.VMEM((seq, qcols), BF16),
+            pltpu.VMEM((seq, qcols), BF16),
+            block, block, block, block, block, block, wide, wide,
+            pltpu.VMEM((1, qcols), F32),
+            pltpu.VMEM((ndp, 1, qcols), F32),
+            pltpu.VMEM((1, d), F32),
+            pltpu.VMEM((n_tensor, 1, d), F32),
+            dma((2, kc)), dma((nc,)), dma((2,)),
+            dma((kc,)), dma((kc,)), dma((kc,)), dma((kc,)), dma((kc,)), dma((kc,)),
+            dma((kvcols // HD, 2)), dma((2, 2)),
+            dma((nc,)), dma((nc,)), dma((nc,)), dma((nc,)), dma((nc,)), dma((nc,)),
+            dma((ndp,)), dma((ndp,)), dma((n_tensor,)), dma((n_tensor,)),
+        ],
+        compiler_params=pltpu.CompilerParams(
+            collective_id=0, has_side_effects=True, vmem_limit_bytes=60 * 1024 * 1024
+        ),
+    )(
+        tokens.reshape(rows, d), gain.reshape(1, d), wq, bq.reshape(1, qcols), wkv,
+        bkv.reshape(1, kvcols), wo, check_weights, cosine, sine,
+    )
+    return attended.reshape(1, rows, d), checksum.reshape(d)
 
 
 def solution(mesh):
@@ -102,6 +495,14 @@
         P("tensor", None),
         P("dp", None),
     )
+    ndp, n_tensor = mesh.shape["dp"], mesh.shape["tensor"]
+
+    def local(tokens, gain, wq, bq, wkv, bkv, wo, check_weights):
+        whole_heads = wkv.shape[1] == 2 * HD and wq.shape[1] == HEADS // KV * HD
+        if n_tensor == KV and whole_heads:
+            return fused(ndp, n_tensor, tokens, gain, wq, bq, wkv, bkv, wo, check_weights)
+        return general(tokens, gain, wq, bq, wkv, bkv, wo, check_weights)
+
     return jax.shard_map(
         local, mesh=mesh, in_specs=placed, out_specs=(P("dp", "tensor", None), P()), check_vma=False
     )

time: 118 us -> 53 us (0.45)
  blocking collectives: 46.9 us -> 0 us
  Pallas kernels: 0 us -> 45 us
  matrix products: 25.1 us -> 0 us
  waiting for transfers between devices: 24.8 us -> 0 us
  between operations: 14.2 us -> 0.64 us
  local copies, waits for them, and re-layouts: 0.68 us -> 7.02 us
  other arithmetic: 6.25 us -> 0 us
    pallas_call x0 -> x1, Pallas kernels: none -> 45 us  [fused(): pl.pallas_call(functools.partial(fused_kernel, ndp, kc, nc), out_shape=(j...]
    psum x1 -> x0, blocking collectives: 39.7 us -> none  [local(): total = lax.psum(term, ('dp', 'tensor'))]
    all_gather x1 -> x0, waiting for transfers between devices: 24.8 us -> none  [local(): lax.all_gather(normed, 'tensor', axis=0, tiled=True)]
    dot_general x5 -> x0, matrix products: 22.8 us -> none  [the longest x1 7.53 us: local(): jnp.dot(lax.all_gather(normed, 'tensor', axis=0, tiled=True), joined_w, p...]
    all_gather x1 -> x0, blocking collectives: 7.16 us -> none  [local(): kv_whole = lax.all_gather(kv_local, 'tensor', axis=1, tiled=True)]
    reshape x0 -> x3, local copies, waits for them, and re-layouts: none -> 3.83 us  [the longest x1 1.31 us: fused(): gain.reshape(1, d)]
    convert_element_type x3 -> x0, other arithmetic: 2.88 us -> none  [the longest x1 2.03 us: local(): normed = (states * lax.rsqrt(jnp.mean(states * states, axis=-1, keepdims=...]
    unnamed x10 -> x2, local copies, waits for them, and re-layouts: 0.33 us -> 3.19 us
  transfers between devices with their start and end apart: 2 -> 0, of which waited for: 1 -> 0; matrix products, arithmetic and copies ran while one was open for 6% -> 0% of each run, Pallas kernels for 0% -> 0%
where the time goes in v1:
time: 53 us; the launch traced here: 52.7 us
  Pallas kernels  45 us (85%)
  local copies, waits for them, and re-layouts  7.02 us (13%)
  between operations  0.64 us (1%)
    pallas_call x1, Pallas kernels, fused(): pl.pallas_call(functools.partial(fused_kernel, ndp, kc, nc), out_shape=(j...  45 us
    unnamed x2, local copies, waits for them, and re-layouts  3.19 us
    reshape x1, local copies, waits for them, and re-layouts, fused(): gain.reshape(1, d)  1.31 us
    reshape x1, local copies, waits for them, and re-layouts, fused(): bq.reshape(1, qcols)  1.28 us
    reshape x1, local copies, waits for them, and re-layouts, fused(): bkv.reshape(1, kvcols)  1.24 us

profile of v1, /device:TPU:0, one launch (start us, length us, event | category | flops | bytes accessed | tf_op | source)
XLA Modules:
  0.0 52.7 jit_solution(16089849171843523407)
XLA Ops:
  0.6 1.2 %reshape.25.bkv = bf16[1,256]{1,0:T(2,128)(2,1)} reshape(bf16[256]{0:T(256)(128)(2,1)} %param.15) | data formatting | bytes 1024 | tf_op jit(solution)/shard_map/reshape | solution.py:482
  1.9 1.3 %reshape.24.bq = bf16[1,1024]{1,0:T(2,128)(2,1)} reshape(bf16[1024]{0:T(1024)(128)(2,1)} %param.13) | data formatting | bytes 4096 | tf_op jit(solution)/shard_map/reshape | solution.py:481
  3.1 1.3 %reshape.23.gain = bf16[1,4096]{1,0:T(2,128)(2,1)} reshape(bf16[4096]{0:T(1024)(128)(2,1)} %param.11) | data formatting | bytes 16384 | tf_op jit(solution)/shard_map/reshape | solution.py:481
  4.5 45.0 %shard_map.113 = (bf16[64,4096]{1,0:T(8,128)(2,1)}, f32[1,4096]{1,0:T(1,128)}) custom-call(bf16[64,4096]{1,0:T(8,128)(2,1)} %bitcast.3, bf16[1,4096]{1,0:T(2,128)(2,1)} %reshape.23.gain, bf16[4096,1024]{1,0:T(8,128)(2,1)} %wq.1, bf16[1,1024]{1,0:T(2,128)(2,1)} %reshape.24.bq, bf16[4096,256]{1,0:T(8,128)(2,1)} %wkv.1, bf16[1,256]{1,0:T(2,128)(2,1)} %reshape.25.bkv, ...), custom_call_target="tpu_custom_call" | custom-call | tf_op jit(solution)/shard_map/pallas_call | solution.py:446
  49.5 1.9 %copy.14 = bf16[1,64,4096]{2,1,0:T(8,128)(2,1)} copy(bf16[1,64,4096]{2,1,0:T(8,128)(2,1)} %bitcast.4) | data formatting | bytes 1048576
  51.3 1.3 %copy.15 = f32[4096]{0:T(1024)} copy(f32[4096]{0:T(1024)} %bitcast.5) | data formatting | bytes 32768

commit v2 on v1

--- a/solution.py
+++ b/solution.py
@@ -121,9 +121,9 @@
 
 def fused_kernel(
     ndp, kc, nc,
-    tok, gain, wq, bq, wkv, bkv, wo, cw, cos, sin,
+    tok_h, gain_h, wq, bq_h, wkv, bkv_h, wo, cw_h, cos, sin,
     out, chk,
-    xs, ws, wos, acc, coss, sins, kvl, kvd, keys, ctx, ctxp,
+    tok, gain, bq, bkv, cw, qs, xs, ws, wos, acc, coss, sins, kvl, kvd, keys, ctx, ctxp,
     p_s, p_r, f_s, f_r, q_s, q_r, keep, mine, sum_s, sum_r, term_s, term_r,
     w_sem, wo_sem, t_sem, far_s, far_r, near_s, near_r, fwd_s, fwd_r, kv_s, kv_r,
     ps_s, ps_r, fs_s, fs_r, qs_s, qs_r, sm_s, sm_r, tm_s, tm_r,
@@ -152,10 +152,22 @@
     barrier = pltpu.get_barrier_semaphore()
     for peer in (partner, across, diagonal):
         pl.semaphore_signal(barrier, inc=1, device_id={"tensor": peer}, device_id_type=MESH)
-    for step in range(1, ndp):
-        pl.semaphore_signal(
-            barrier, inc=1, device_id={"dp": (dp + step) % ndp}, device_id_type=MESH
-        )
+    bits = ndp.bit_length() - 1
+
+    def twin(bit):
+        return dp + 2**bit * (1 - 2 * (dp // 2**bit % 2))
+
+    for bit in range(bits):
+        pl.semaphore_signal(barrier, inc=1, device_id={"dp": twin(bit)}, device_id_type=MESH)
+
+    smalls = [
+        pltpu.make_async_copy(source, target, t_sem.at[index])
+        for index, (source, target) in enumerate(
+            ((tok_h, tok), (gain_h, gain), (bq_h, bq), (bkv_h, bkv), (cw_h, cw), (cos, coss), (sin, sins))
+        )
+    ]
+    smalls[0].start()
+    smalls[1].start()
 
     def load_q(k):
         at = pl.ds(k * kch, kch)
@@ -174,13 +186,13 @@
     for k in range(kc):
         load_q(k).start()
         load_kv(k).start()
-    load_cos = pltpu.make_async_copy(cos, coss, t_sem.at[0])
-    load_sin = pltpu.make_async_copy(sin, sins, t_sem.at[1])
-    load_cos.start()
-    load_sin.start()
+    for small in smalls[2:]:
+        small.start()
     for n in range(nc):
         load_o(n).start()
 
+    smalls[0].wait()
+    smalls[1].wait()
     square = jnp.zeros((rows, kch), F32)
     for k in range(kc):
         part = tok[:, k * kch : (k + 1) * kch].astype(F32)
@@ -188,10 +200,10 @@
     inverse = lax.rsqrt(jnp.sum(square, axis=-1, keepdims=True) / d + EPS)
     for k in range(kc):
         part = tok[:, k * kch : (k + 1) * kch].astype(F32)
-        scaled = part * inverse * gain[:, k * kch : (k + 1) * kch].astype(F32)
+        scaled = part * inverse * gain[k * kch : (k + 1) * kch].astype(F32)[None, :]
         xs[k, rows_of(me), :] = scaled.astype(BF16)
 
-    pl.semaphore_wait(barrier, 3 + ndp - 1)
+    pl.semaphore_wait(barrier, 3 + bits)
 
     def remote(src, dst, send, recv, peer):
         return pltpu.make_async_remote_copy(
@@ -215,12 +227,21 @@
         near(k, me).start()
         far(k, me).start()
 
-    def project(k, at, first):
-        product = jnp.dot(xs[k, at, :], ws[k], preferred_element_type=F32)
+    def project(k, at, first, begin=0, end=None):
+        end = ws.shape[2] if end is None else end
+        product = jnp.dot(xs[k, at, :], ws[k, :, begin:end], preferred_element_type=F32)
         if first:
-            acc[at, :] = product
+            acc[at, begin:end] = product
         else:
-            acc[at, :] += product
+            acc[at, begin:end] += product
+
+    def rope_query(half):
+        at = pl.ds(pl.multiple_of(half * pair, pair), pair)
+        for h in range(heads):
+            lanes = slice(h * HD, (h + 1) * HD)
+            query = acc[at, lanes] + bq[lanes].astype(F32)[None, :]
+            query = query * coss[at, :] + pltpu.roll(query, HD // 2, 1) * sins[at, :]
+            qs[at, lanes] = query.astype(BF16)
 
     def own_step(k, first):
         load_q(k).wait()
@@ -253,7 +274,7 @@
         at = pl.ds(pl.multiple_of(half * pair, pair), pair)
         for slot in range(kinds):
             lanes = slice(qcols + slot * HD, qcols + (slot + 1) * HD)
-            bias = bkv[:, slot * HD : (slot + 1) * HD].astype(F32)
+            bias = bkv[slot * HD : (slot + 1) * HD].astype(F32)[None, :]
             kvl[slot, at, :] = (acc[at, lanes] + bias).astype(BF16)
         for slot in range(kinds):
             number = me * kinds + slot
@@ -266,19 +287,26 @@
             def _():
                 kvd[number // KV, at, :] = kvl[slot, at, :]
 
+    for small in smalls[2:]:
+        small.wait()
     kv_send(chip)
 
     for k in range(kc + 1):
         if k < kc:
             far(k, across).wait_recv()
             forward(k, across).start()
+        if k == 1:
+            rope_query(chip)
         if k > 0:
             forward(k - 1, diagonal).wait_recv()
-            project(k - 1, other_rows, k == 1)
+            if k < kc:
+                project(k - 1, other_rows, k == 1)
+            else:
+                project(k - 1, other_rows, k == 1, qcols)
     kv_send(1 - chip)
-
-    load_cos.wait()
-    load_sin.wait()
+    project(kc - 1, other_rows, False, 0, qcols)
+    rope_query(1 - chip)
+
     shared = me * heads // (HEADS // KV)
     for kind in range(2):
         source = (kind * KV + shared) // kinds
@@ -292,29 +320,28 @@
     keys[...] = (raw * coss[...] + pltpu.roll(raw, HD // 2, 1) * sins[...]).astype(BF16)
 
     scale = HD ** (-0.5)
-    for h in range(heads):
-        lanes = slice(h * HD, (h + 1) * HD)
-        for block in range(2):
-            at = slice(block * pair, (block + 1) * pair)
-            stop = (block + 1) * pair
-            query = acc[at, lanes] + bq[:, lanes].astype(F32)
-            query = query * coss[at, :] + pltpu.roll(query, HD // 2, 1) * sins[at, :]
+
+    def attend(block):
+        at = pl.ds(pl.multiple_of(block * pair, pair), pair)
+        same = 1 - (block - chip) * (block - chip)
+        for h in range(heads):
+            lanes = slice(h * HD, (h + 1) * HD)
             scores = lax.dot_general(
-                query.astype(BF16), keys[:stop, :], (((1,), (1,)), ((), ())),
-                preferred_element_type=F32,
+                qs[at, lanes], keys[...], (((1,), (1,)), ((), ())), preferred_element_type=F32
             ) * scale
             down = lax.broadcasted_iota(jnp.int32, scores.shape, 0) + block * pair
             right = lax.broadcasted_iota(jnp.int32, scores.shape, 1)
             scores = jnp.where(down >= right, scores, -1e30)
             raised = jnp.exp(scores - jnp.max(scores, axis=-1, keepdims=True))
             total = jnp.sum(raised, axis=-1, keepdims=True)
-            mixed = jnp.dot(raised.astype(BF16), kvd[1, :stop, :], preferred_element_type=F32)
+            mixed = jnp.dot(raised.astype(BF16), kvd[1, :, :], preferred_element_type=F32)
             mixed = (mixed * (1.0 / total)).astype(BF16)
             ctx[at, lanes] = mixed
-            same = 1 - (block - chip) * (block - chip)
             for side in range(2):
                 place = 2 * same + 1 - (side - core) * (side - core)
                 ctxp[rows_of(place), lanes] = mixed[side * rows : (side + 1) * rows, :]
+
+    attend(1 - chip)
 
     def p_copy(n):
         return remote(p_s.at[n], p_r.at[n], ps_s.at[n], ps_r.at[n], partner)
@@ -337,54 +364,55 @@
         p_copy(n).start()
         keep[n] = product[rows:]
 
-    first_part(0)
-
-    @pl.loop(1, nc)
-    def _(n):
-        first_part(n)
-        cross(n - 1)
-
-    weighted = jnp.dot(split3(cw[...]), ctx[...], preferred_element_type=F32)
-    summary = jnp.sum(weighted, axis=0, keepdims=True)
-    sum_s[...] = summary
-    sum_r[dp] = summary
-    cross(nc - 1)
-
-    def sum_copy(peer, owner):
+    def sum_copy(bit):
         return pltpu.make_async_remote_copy(
-            src_ref=sum_s, dst_ref=sum_r.at[owner], send_sem=sm_s.at[peer],
-            recv_sem=sm_r.at[owner], device_id={"dp": peer}, device_id_type=MESH,
-        )
-
-    for step in range(1, ndp):
-        sum_copy((dp + step) % ndp, dp).start()
-
-    @pl.loop(0, nc)
-    def _(n):
+            src_ref=sum_s.at[bit], dst_ref=sum_r.at[bit], send_sem=sm_s.at[bit],
+            recv_sem=sm_r.at[bit], device_id={"dp": twin(bit)}, device_id_type=MESH,
+        )
+
+    def own_part(n):
         product = jnp.dot(ctxp[pair:, :], wos[n], preferred_element_type=F32)
         q_s[n] = product[:rows].astype(BF16)
         q_copy(n).start()
         mine[n] = product[rows:]
 
-    for step in range(1, ndp):
-        peer = (dp + step) % ndp
-        sum_copy(peer, peer).wait_recv()
-    whole = sum_r[0]
-    for index in range(1, ndp):
-        whole = whole + sum_r[index]
+    lead = 3
+    first_part(0)
+    for n in range(1, lead):
+        first_part(n)
+        cross(n - 1)
+    attend(chip)
+    weighted = jnp.dot(split3(cw[...]), ctx[...], preferred_element_type=F32)
+    whole = jnp.sum(weighted, axis=0, keepdims=True)
+    edges = [lead + (nc - lead) * step // bits for step in range(bits + 1)]
+    for bit in range(bits):
+        sum_s[bit] = whole
+        sum_copy(bit).start()
+        for n in range(edges[bit], edges[bit + 1]):
+            first_part(n)
+            cross(n - 1)
+        if bit == bits - 1:
+            cross(nc - 1)
+        sum_copy(bit).wait_recv()
+        whole = whole + sum_r[bit]
+
+    def term_copy(step):
+        return remote(
+            term_s.at[step], term_r.at[step], tm_s.at[step], tm_r.at[step],
+            (partner, across)[step],
+        )
+
     three = split3(whole)
     for n in range(nc):
         lanes = slice(n * nch, (n + 1) * nch)
         product = jnp.dot(three, wos[n], preferred_element_type=F32)
-        term = jnp.sum(product, axis=0, keepdims=True)
-        term_s[:, lanes] = term
-        term_r[me, :, lanes] = term
-
-    def term_copy(peer, owner):
-        return remote(term_s, term_r.at[owner], tm_s.at[peer], tm_r.at[owner], peer)
-
-    for peer in (partner, across, diagonal):
-        term_copy(peer, me).start()
+        term_s[0, :, lanes] = jnp.sum(product, axis=0, keepdims=True)
+    term_copy(0).start()
+    pl.loop(0, nc // 2)(own_part)
+    term_copy(0).wait_recv()
+    term_s[1] = term_s[0] + term_r[0]
+    term_copy(1).start()
+    pl.loop(nc // 2, nc)(own_part)
 
     for n in range(nc):
         lanes = slice(n * nch, (n + 1) * nch)
@@ -392,11 +420,9 @@
         f_copy(n).wait_recv()
         out[:, lanes] = (mine[n] + q_r[n].astype(F32) + f_r[n].astype(F32)).astype(BF16)
 
-    for peer in (partner, across, diagonal):
-        term_copy(peer, peer).wait_recv()
+    term_copy(1).wait_recv()
     size = np.float32(1.0) / np.sqrt(np.float32(seq * ndp))
-    total = term_r[0] + term_r[1] + term_r[2] + term_r[3]
-    chk[...] = total * size
+    chk[...] = (term_s[1] + term_r[1]) * size
 
     for k in range(kc):
         near(k, me).wait_send()
@@ -413,10 +439,15 @@
         p_copy(n).wait_send()
         f_copy(n).wait_send()
         q_copy(n).wait_send()
-    for step in range(1, ndp):
-        sum_copy((dp + step) % ndp, dp).wait_send()
-    for peer in (partner, across, diagonal):
-        term_copy(peer, me).wait_send()
+    for bit in range(bits):
+        sum_copy(bit).wait_send()
+    for step in range(2):
+        term_copy(step).wait_send()
+
+
+def settle_kernel(attended, checksum, out, chk):
+    out[...] = attended[...]
+    chk[...] = checksum[...].reshape(chk.shape)
 
 
 def tables(seq):
@@ -439,19 +470,26 @@
     qcols, kvcols = wq.shape[1], wkv.shape[1]
     cosine, sine = tables(seq)
     vmem = pl.BlockSpec(memory_space=pltpu.VMEM)
-    hbm = pl.BlockSpec(memory_space=pl.ANY)
+    hbm = pl.BlockSpec(memory_space=pltpu.HBM)
     dma = pltpu.SemaphoreType.DMA
     block = pltpu.VMEM((nc, rows, nch), BF16)
     wide = pltpu.VMEM((nc, rows, nch), F32)
+    bits = ndp.bit_length() - 1
     attended, checksum = pl.pallas_call(
         functools.partial(fused_kernel, ndp, kc, nc),
         out_shape=(
             jax.ShapeDtypeStruct((rows, d), BF16),
             jax.ShapeDtypeStruct((1, d), F32),
         ),
-        in_specs=[vmem, vmem, hbm, vmem, hbm, vmem, hbm, vmem, hbm, hbm],
+        in_specs=[hbm] * 10,
         out_specs=(vmem, vmem),
         scratch_shapes=[
+            pltpu.VMEM((rows, d), BF16),
+            pltpu.VMEM((d,), BF16),
+            pltpu.VMEM((qcols,), BF16),
+            pltpu.VMEM((kvcols,), BF16),
+            pltpu.VMEM((1, seq), F32),
+            pltpu.VMEM((seq, qcols), BF16),
             pltpu.VMEM((kc, seq, kch), BF16),
             pltpu.VMEM((kc, kch, qcols + kvcols), BF16),
             pltpu.VMEM((nc, qcols, nch), BF16),
@@ -464,24 +502,29 @@
             pltpu.VMEM((seq, qcols), BF16),
             pltpu.VMEM((seq, qcols), BF16),
             block, block, block, block, block, block, wide, wide,
-            pltpu.VMEM((1, qcols), F32),
-            pltpu.VMEM((ndp, 1, qcols), F32),
-            pltpu.VMEM((1, d), F32),
-            pltpu.VMEM((n_tensor, 1, d), F32),
-            dma((2, kc)), dma((nc,)), dma((2,)),
+            pltpu.VMEM((bits, 1, qcols), F32),
+            pltpu.VMEM((bits, 1, qcols), F32),
+            pltpu.VMEM((2, 1, d), F32),
+            pltpu.VMEM((2, 1, d), F32),
+            dma((2, kc)), dma((nc,)), dma((7,)),
             dma((kc,)), dma((kc,)), dma((kc,)), dma((kc,)), dma((kc,)), dma((kc,)),
             dma((kvcols // HD, 2)), dma((2, 2)),
             dma((nc,)), dma((nc,)), dma((nc,)), dma((nc,)), dma((nc,)), dma((nc,)),
-            dma((ndp,)), dma((ndp,)), dma((n_tensor,)), dma((n_tensor,)),
+            dma((bits,)), dma((bits,)), dma((2,)), dma((2,)),
         ],
         compiler_params=pltpu.CompilerParams(
-            collective_id=0, has_side_effects=True, vmem_limit_bytes=60 * 1024 * 1024
+            collective_id=0, has_side_effects=True, vmem_limit_bytes=63300000
         ),
     )(
-        tokens.reshape(rows, d), gain.reshape(1, d), wq, bq.reshape(1, qcols), wkv,
-        bkv.reshape(1, kvcols), wo, check_weights, cosine, sine,
-    )
-    return attended.reshape(1, rows, d), checksum.reshape(d)
+        tokens.reshape(rows, d), gain, wq, bq, wkv, bkv, wo, check_weights, cosine, sine,
+    )
+    attended, checksum = pl.pallas_call(
+        settle_kernel,
+        out_shape=(jax.ShapeDtypeStruct((rows, d), BF16), jax.ShapeDtypeStruct((d,), F32)),
+        in_specs=[vmem, vmem],
+        out_specs=(vmem, vmem),
+    )(attended, checksum)
+    return attended.reshape(1, rows, d), checksum
 
 
 def solution(mesh):
@@ -499,7 +542,7 @@
 
     def local(tokens, gain, wq, bq, wkv, bkv, wo, check_weights):
         whole_heads = wkv.shape[1] == 2 * HD and wq.shape[1] == HEADS // KV * HD
-        if n_tensor == KV and whole_heads:
+        if n_tensor == KV and whole_heads and ndp & (ndp - 1) == 0:
             return fused(ndp, n_tensor, tokens, gain, wq, bq, wkv, bkv, wo, check_weights)
         return general(tokens, gain, wq, bq, wkv, bkv, wo, check_weights)
 

time: 53 us -> 47.5 us (0.90)
  local copies, waits for them, and re-layouts: 7.02 us -> 0 us
  Pallas kernels: 45 us -> 46.7 us
    reshape x3 -> x0, local copies, waits for them, and re-layouts: 3.83 us -> none  [the longest x1 1.31 us: fused(): gain.reshape(1, d)]
    unnamed x2 -> x0, local copies, waits for them, and re-layouts: 3.19 us -> none
    pallas_call x0 -> x1, Pallas kernels: none -> 1.87 us  [fused(): pl.pallas_call(settle_kernel, out_shape=(jax.ShapeDtypeStruct((rows, d),...]
where the time goes in v2:
time: 47.5 us; the launch traced here: 47.3 us
  Pallas kernels  46.7 us (98%)
  between operations  0.64 us (1%)
    pallas_call x1, Pallas kernels, fused(): pl.pallas_call(functools.partial(fused_kernel, ndp, kc, nc), out_shape=(j...  44.8 us
    pallas_call x1, Pallas kernels, fused(): pl.pallas_call(settle_kernel, out_shape=(jax.ShapeDtypeStruct((rows, d),...  1.87 us

profile of v2, /device:TPU:0, one launch (start us, length us, event | category | flops | bytes accessed | tf_op | source)
XLA Modules:
  0.0 47.3 jit_solution(5427523255903513195)
XLA Ops:
  0.6 44.8 %shard_map.113 = (bf16[64,4096]{1,0:T(8,128)(2,1)}, f32[1,4096]{1,0:T(1,128)}) custom-call(bf16[64,4096]{1,0:T(8,128)(2,1)} %bitcast.2, bf16[4096]{0:T(1024)(128)(2,1)} %gain_h.1, bf16[4096,1024]{1,0:T(8,128)(2,1)} %wq.1, bf16[1024]{0:T(1024)(128)(2,1)} %bq_h.1, bf16[4096,256]{1,0:T(8,128)(2,1)} %wkv.1, bf16[256]{0:T(256)(128)(2,1)} %bkv_h.1, ...), custom_call_target="tpu_custom_call" | custom-call | tf_op jit(solution)/shard_map/pallas_call | solution.py:478
  45.4 1.9 %shard_map.114 = (bf16[64,4096]{1,0:T(8,128)(2,1)}, f32[4096]{0:T(1024)}) custom-call(bf16[64,4096]{1,0:T(8,128)(2,1)} %get-tuple-element.6.attended, f32[1,4096]{1,0:T(1,128)} %get-tuple-element.7.checksum), custom_call_target="tpu_custom_call" | custom-call | tf_op jit(solution)/shard_map/pallas_call | solution.py:521
